TPU v7x, 32 devices: a whole 2x2x4 slice. The times are simulated.
32 devices in a mesh: dom: 16 (over z, y, x), field: 2 (over core).
Axes of the slice: x: 2, y: 2, z: 4, core: 2. Of those that a mesh axis runs over, the one named last changes fastest.
Arguments:
- ocean: bfloat16 [30, 32768], P('field', 'dom'), may hold values from -6 to 6
- grad_weight: bfloat16 [256, 4, 128, 256], P('dom'), may hold values from -0.25 to 0.25
- neighbours: int32 [256, 4], P('dom'), may hold values from 0 to 255, as said below
- remap_weight: bfloat16 [2048, 384, 128], P(('dom', 'field')), may hold values from -0.109375 to 0.109375
- tile_src: int32 [2048], P(('dom', 'field')), may hold values from 0 to 255, as said below
- tile_atm: int32 [2048], P(('dom', 'field')), may hold values from 0 to 255, as said below
- atm_owner: int32 [256], replicated, may hold values from 0 to 255, as said below
Outputs:
- atmosphere: float32 [30, 32768], P('field', 'dom')
Inputs may be any that keep to these rules, and one draw needn't show every extreme that they name: `neighbours`: the stencil of a block of partition p holds blocks of p, the last 2 blocks of partition p - 1 or the first 2 blocks of partition p + 1 (partitions are the aligned runs of 16 blocks; no wrap). `tile_src`: tile t names a block of partition t // 128, the partition that holds the tile. `tile_atm`: of the aligned runs of 64 tiles, no run has more than 16 tiles whose atmosphere tile has owner position in one aligned run of 16; in every draw each run reaches 16 for some owner. `atm_owner`: A permutation of the atmosphere tiles.
All inputs are finite; a program needn't handle non-finite values.
Results may differ from a plain program's by a relative error of at most 0.0042.
Values may be sent and summed in bfloat16 or wider, within the bound.
A program may use at most 64 MiB of HBM per device.

v0:
```python
import jax
import jax.numpy as jnp
from jax import lax
from jax.sharding import PartitionSpec as P


def padded_2(shard, sides, width):
    for axis, dim in sides:
        size, length = (lax.axis_size(axis), shard.shape[dim])
        up = [(i, (i + 1) % size) for i in range(size - 1)]
        down = [(j, i) for i, j in up]
        last = lax.slice_in_dim(shard, length - width, length, axis=dim)
        initial = lax.slice_in_dim(shard, 0, width, axis=dim)
        before = lax.ppermute(last, axis, up)
        after = lax.ppermute(initial, axis, down)
        shard = jnp.concatenate([before, shard, after], axis=dim)
    return shard


def deliver(contribution, target_dev, local_slot, devices, capacity, owned):
    tile_count = target_dev.shape[0]
    tile_order = jnp.arange(tile_count, dtype=jnp.int32)
    before = jnp.sum(
        (
            (target_dev[:, None] == target_dev[None, :])
            & (tile_order[None, :] < tile_order[:, None])
        ).astype(jnp.int32),
        axis=1,
    )
    position = target_dev * capacity + before
    slot_count = devices * capacity
    matches = position[None, :] == jnp.arange(slot_count, dtype=jnp.int32)[:, None]
    chosen = jnp.sum(jnp.where(matches, tile_order[None, :], 0), axis=1)
    filled = jnp.any(matches, axis=1)
    outgoing = jnp.where(filled[:, None, None], contribution[chosen], 0.0)
    targets = jnp.where(filled, local_slot[chosen], -1)
    incoming, in_targets = (
        lax.all_to_all(outgoing, "dom", split_axis=0, concat_axis=0, tiled=True),
        lax.all_to_all(targets, "dom", split_axis=0, concat_axis=0, tiled=True),
    )
    selector = (in_targets[None, :] == jnp.arange(owned, dtype=jnp.int32)[:, None]).astype(
        jnp.float32
    )
    summed = jnp.einsum("ak,kfc->fac", selector, incoming, precision=lax.Precision.HIGHEST)
    return summed.reshape(summed.shape[0], owned * summed.shape[2])


def local(ocean, grad_weight, neighbours, remap_weight, tile_src, tile_atm, atm_owner):
    block_len = grad_weight.shape[2]
    field_rows = ocean.shape[0]
    nblocks = grad_weight.shape[0]
    device = lax.axis_index("dom")
    devices = lax.axis_size("dom")
    per_core = tile_atm.shape[0]
    capacity_base = max(2, 4 * per_core // devices)
    padded = padded_2(ocean, (("dom", 1),), nblocks * block_len)
    first_block = device * nblocks - nblocks
    extended = padded.reshape(field_rows, -1, block_len)
    local_ids = neighbours - first_block
    picked = jnp.take(extended, local_ids, axis=1)
    gradient = jnp.einsum(
        "fbkj,bkjo->fbo", picked, grad_weight, preferred_element_type=jnp.float32
    ).astype(jnp.bfloat16)
    source = jnp.concatenate([ocean.reshape(field_rows, nblocks, block_len), gradient], axis=2)
    source = lax.all_gather(source, "field", axis=0, tiled=True)
    local_src = tile_src - device * nblocks
    source_rows = jnp.take(source, local_src, axis=1)
    contribution = jnp.einsum(
        "ftj,tjc->tfc", source_rows, remap_weight, preferred_element_type=jnp.float32
    )
    atm_tiles = atm_owner.shape[0]
    atm_slot = jnp.sum(
        jnp.where(
            tile_atm[:, None] == jnp.arange(atm_tiles, dtype=jnp.int32)[None, :],
            atm_owner[None, :],
            0,
        ),
        axis=1,
    )
    owned = atm_tiles // devices
    target_dev = atm_slot // owned
    local_slot = atm_slot % owned
    summed = deliver(contribution, target_dev, local_slot, devices, capacity_base, owned)
    return lax.psum_scatter(summed, "field", scatter_dimension=0, tiled=True)


def solution(mesh):
    in_specs = (
        P("field", "dom"),
        P("dom", None, None, None),
        P("dom", None),
        P(("dom", "field"), None, None),
        P(("dom", "field")),
        P(("dom", "field")),
        P(),
    )
    out_specs = P("field", "dom")
    return jax.shard_map(local, mesh=mesh, in_specs=in_specs, out_specs=out_specs, check_vma=False)
```

profile of v0, /device:TPU:15, one launch (start us, length us, event | category | flops | bytes accessed | tf_op | source)
XLA Modules:
  0.0 153.9 jit_solution(14185718574713229053)
XLA Ops:
  0.0 3.1 %collective-permute-start = (bf16[15,2048]{1,0:T(8,128)(2,1)}, bf16[15,2048]{1,0:T(8,128)(2,1)S(1)}, u32[]{:S(2)}, u32[]{:S(2)}) collective-permute-start(bf16[15,2048]{1,0:T(8,128)(2,1)} %param.7), channel_id=1, source_target_pairs={{0,2},{2,4},{4,6},{6,8},{8,10},{10,12},{12,14},{14,16},{16,18},{18... | collective-permute-start | bytes 184328 | tf_op jit(solution)/shard_map/ppermute | solution.py:14
  3.1 2.2 %collective-permute-start.1 = (bf16[15,2048]{1,0:T(8,128)(2,1)}, bf16[15,2048]{1,0:T(8,128)(2,1)S(1)}, u32[]{:S(2)}, u32[]{:S(2)}) collective-permute-start(bf16[15,2048]{1,0:T(8,128)(2,1)} %param.7), channel_id=1, source_target_pairs={{2,0},{4,2},{6,4},{8,6},{10,8},{12,10},{14,12},{16,14},{18,16},{20... | collective-permute-start | bytes 184328 | tf_op jit(solution)/shard_map/ppermute | solution.py:15
  5.3 0.9 select_reduce_fusion.1
  6.2 0.2 convert_reduce_fusion
  6.4 0.1 fusion.17
  6.5 0.1 select_reduce_fusion
  6.6 1.9 %gather_fusion.3 = s32[256]{0:T(256)S(1)} fusion(s32[64]{0:T(128)S(1)} %get-tuple-element.9, s32[1024]{0:T(1024)S(1)} %pad_clamp_fusion), kind=kCustom, calls=%fused_computation.3 | custom fusion | bytes 3072 | tf_op jit(solution)/shard_map/gather | solution.py:36
  8.5 0.7 select_n.88
  9.2 6.6 %all-to-all-start.1 = ((s32[16,16,1]{1,2,0:T(1,128)}), s32[16,16,1]{1,2,0:T(1,128)S(1)}, u32[]{:S(2)}, u32[]{:S(2)}) async-start(s32[16,16,1]{1,2,0:T(1,128)} %bitcast.8), calls=%async_computation.1 | async-start | bytes 16384 | tf_op jit(solution)/shard_map/all_to_all | solution.py:39
  15.7 0.7 compare_and_fusion.1
  16.4 0.7 compare_and_fusion
  17.1 0.1 copy.40
  17.2 0.1 copy.41
  17.3 0.1 reshape.103
  17.4 0.9 copy.49
  18.3 0.0 collective-permute-done
  18.3 0.0 collective-permute-done.1
  18.3 0.9 pad_maximum_fusion
  19.2 0.1 copy.42
  19.3 0.6 gather_fusion
  19.9 2.9 %fusion.11 = bf16[15,16,256]{2,0,1:T(8,128)(2,1)S(1)} fusion(bf16[16,4,128,256]{3,2,1,0:T(8,128)(2,1)} %param.8, bf16[16,4,15,128]{3,2,1,0:T(8,128)(2,1)S(1)} %bitcast.41, pred[16,4]{1,0:T(8,128)(4,1)S(1)} %copy.40), kind=kOutput, calls=%fused_computation.14 | convolution fusion | flops 63098880 | bytes 4563008 | tf_op jit(solution)/shard_map/fbkj,bkjo->fbo/dot_general | solution.py:61
  22.9 3.5 %all_gather.3 = bf16[30,16,384]{2,1,0:T(8,128)(2,1)S(1)} all-gather(bf16[15,16,384]{2,1,0:T(8,128)(2,1)S(1)} %copy.44), channel_id=1, replica_groups=mesh['dom'=16,'field'=2] {'field'}, dimensions={0}, use_global_device_ids=true | all-gather | bytes 552960 | tf_op jit(solution)/shard_map/all_gather | solution.py:65
  26.4 0.1 copy.45
  26.5 0.9 gather_fusion.1
  27.3 4.0 %fusion.3 = f32[64,30,128]{2,1,0:T(8,128)S(1)} fusion(bf16[64,384,128]{2,1,0:T(8,128)(2,1)} %param.10, bf16[64,30,384]{2,1,0:T(8,128)(2,1)S(1)} %gather_fusion.1, pred[64]{0:T(512)(128)(4,1)S(1)} %get-tuple-element.5), kind=kOutput, calls=%fused_computation.7 | convolution fusion | flops 189480960 | bytes 8749120 | tf_op jit(solution)/shard_map/ftj,tjc->tfc/dot_general | solution.py:68
  31.4 3.0 %gather_fusion.2 = f32[256,30,128]{2,1,0:T(8,128)} fusion(f32[64,30,128]{2,1,0:T(8,128)S(1)} %fusion.3, s32[1024]{0:T(1024)S(1)} %pad_clamp_fusion), kind=kCustom, calls=%fused_computation.2 | custom fusion | bytes 7865344 | tf_op jit(solution)/shard_map/gather | solution.py:35
  34.4 4.0 %broadcast_select_fusion = f32[256,30,128]{2,1,0:T(8,128)} fusion(f32[256,30,128]{2,1,0:T(8,128)} %gather_fusion.2, pred[256]{0:T(512)(128)(4,1)S(1)} %fusion.17), kind=kLoop, calls=%fused_computation.6 | loop fusion | flops 983040 | bytes 7864576 | tf_op jit(solution)/shard_map/jit(_where)/select_n | solution.py:35
  38.4 0.0 all-to-all-done.1
  38.4 6.4 %all-to-all-start = ((f32[256,30,128]{2,1,0:T(8,128)}), f32[256,30,128]{2,1,0:T(8,128)}, u32[]{:S(2)}, u32[]{:S(2)}) async-start(f32[256,30,128]{2,1,0:T(8,128)} %broadcast_select_fusion), calls=%async_computation | async-start | bytes 8388608 | tf_op jit(solution)/shard_map/all_to_all | solution.py:38
  44.8 0.0 copy-start
  44.8 0.5 broadcast.180
  45.3 0.7 reduce.3
  46.0 0.1 eq.65
  46.1 93.8 %all-to-all-done = f32[256,30,128]{2,1,0:T(8,128)} async-done(((f32[256,30,128]{2,1,0:T(8,128)}), f32[256,30,128]{2,1,0:T(8,128)}, u32[]{:S(2)}, u32[]{:S(2)}) %all-to-all-start) | async-done | bytes 3932192 | tf_op jit(solution)/shard_map/all_to_all | solution.py:38
  139.9 5.6 %fusion.7 = f32[30,16,128]{2,1,0:T(8,128)S(1)} fusion(f32[256,30,128]{2,1,0:T(8,128)} %all-to-all-done, s32[256]{0:T(256)S(1)} %eq.65), kind=kOutput, calls=%fused_computation.12 | convolution fusion | flops 188747776 | bytes 4178944 | tf_op jit(solution)/shard_map/ak,kfc->fac/dot_general | solution.py:44
  145.5 0.1 copy.51
  145.6 4.3 %fusion = f32[16,2048]{1,0:T(8,128)S(1)} fusion(f32[30,2048]{1,0:T(8,128)S(1)} %bitcast.40), kind=kCustom, calls=%all-reduce-scatter | all-reduce-scatter fusion | flops 65537 | bytes 377344
  149.9 1.3 collective-permute-start.2
  151.2 0.0 copy-done
  151.3 0.6 dynamic-slice.4
  152.5 0.5 collective-permute-done.2
  153.0 0.2 concatenate.8
  153.2 0.7 constant_dynamic-slice_fusion
  (15 shorter events, 0.2 us)
Async XLA Ops:
  0.0 18.3 %collective-permute-start = (bf16[15,2048]{1,0:T(8,128)(2,1)}, bf16[15,2048]{1,0:T(8,128)(2,1)S(1)}, u32[]{:S(2)}, u32[]{:S(2)}) collective-permute-start(bf16[15,2048]{1,0:T(8,128)(2,1)} %param.7), channel_id=1, source_target_pairs={{0,2},{2,4},{4,6},{6,8},{8,10},{10,12},{12,14},{14,16},{16,18},{18... | collective-permute-start | bytes 184328 | tf_op jit(solution)/shard_map/ppermute | solution.py:14
  3.1 15.2 %collective-permute-start.1 = (bf16[15,2048]{1,0:T(8,128)(2,1)}, bf16[15,2048]{1,0:T(8,128)(2,1)S(1)}, u32[]{:S(2)}, u32[]{:S(2)}) collective-permute-start(bf16[15,2048]{1,0:T(8,128)(2,1)} %param.7), channel_id=1, source_target_pairs={{2,0},{4,2},{6,4},{8,6},{10,8},{12,10},{14,12},{16,14},{18,16},{20... | collective-permute-start | bytes 184328 | tf_op jit(solution)/shard_map/ppermute | solution.py:15
  9.2 29.3 %all-to-all-start.1 = ((s32[16,16,1]{1,2,0:T(1,128)}), s32[16,16,1]{1,2,0:T(1,128)S(1)}, u32[]{:S(2)}, u32[]{:S(2)}) async-start(s32[16,16,1]{1,2,0:T(1,128)} %bitcast.8), calls=%async_computation.1 | async-start | bytes 16384 | tf_op jit(solution)/shard_map/all_to_all | solution.py:39
  38.4 101.5 %all-to-all-start = ((f32[256,30,128]{2,1,0:T(8,128)}), f32[256,30,128]{2,1,0:T(8,128)}, u32[]{:S(2)}, u32[]{:S(2)}) async-start(f32[256,30,128]{2,1,0:T(8,128)} %broadcast_select_fusion), calls=%async_computation | async-start | bytes 8388608 | tf_op jit(solution)/shard_map/all_to_all | solution.py:38
  44.8 106.4 %copy-start = (u32[32]{0:T(128)S(1)}, u32[32]{0:T(128)}, u32[]{:S(2)}) copy-start(u32[32]{0:T(128)} %constant.76) | copy-start | bytes 388
  149.9 3.1 %collective-permute-start.2 = (f32[1,2048]{1,0:T(1,128)S(1)}, f32[1,2048]{1,0:T(1,128)S(1)}, u32[]{:S(2)}, u32[]{:S(2)}) collective-permute-start(f32[1,2048]{1,0:T(1,128)S(1)} %slice.8), channel_id=1, source_target_pairs={{0,1},{2,3},{4,5},{6,7},{8,9},{10,11},{12,13},{14,15},{16,17},{18,... | collective-permute-start | bytes 24584
where the time goes:
time: 154 us
  waiting for transfers between devices  94.3 us (61%)
  starting transfers between devices  19.5 us (13%)
  matrix products  12.5 us (8%)
  local copies, waits for them, and re-layouts  10.6 us (7%)
  other arithmetic  8.22 us (5%)
  blocking collectives  7.79 us (5%)
    all_to_all x1, waiting for transfers between devices, deliver(): lax.all_to_all(outgoing, 'dom', split_axis=0, concat_axis=0, tiled=True)  93.8 us
    all_to_all x1, starting transfers between devices, deliver(): lax.all_to_all(targets, 'dom', split_axis=0, concat_axis=0, tiled=True)  6.58 us
    all_to_all x1, starting transfers between devices, deliver(): lax.all_to_all(outgoing, 'dom', split_axis=0, concat_axis=0, tiled=True)  6.36 us
    dot_general x1, matrix products, deliver(): jnp.einsum('ak,kfc->fac', selector, incoming, precision=lax.Precision.HIG...  5.6 us
    unnamed x1, blocking collectives  4.29 us
    dot_general x1, matrix products, local(): jnp.einsum('ftj,tjc->tfc', source_rows, remap_weight, preferred_element_t...  4.05 us
    select_n x2, other arithmetic, deliver(): outgoing = jnp.where(filled[:, None, None], contribution[chosen], 0.0)  4.03 us
    all_gather x1, blocking collectives, local(): source = lax.all_gather(source, 'field', axis=0, tiled=True)  3.5 us
  transfers between devices with their start and end apart: 5, of which 2 were waited for; matrix products, arithmetic and copies ran while one was open for 16% of the time, Pallas kernels for 0%

commit v1 on v0

--- a/solution.py
+++ b/solution.py
@@ -1,6 +1,10 @@
+import functools
+
 import jax
 import jax.numpy as jnp
 from jax import lax
+from jax.experimental import pallas as pl
+from jax.experimental.pallas import tpu as pltpu
 from jax.sharding import PartitionSpec as P
 
 
@@ -84,6 +88,338 @@
     return lax.psum_scatter(summed, "field", scatter_dimension=0, tiled=True)
 
 
+HALO = 2
+MESH = pl.DeviceIdType.MESH
+
+
+def stage_masks(stages, core):
+    masks = [jnp.int32(1 << s) for s in range(stages)]
+    if stages >= 2:
+        masks[0] = jnp.where(core == 0, 1, 2)
+        masks[1] = jnp.where(core == 0, 2, 1)
+    return masks
+
+
+def fused_kernel(
+    devices, stages, owned, groups,
+    ocean, neighbours, tile_src, tile_atm, atm_owner, grad_weight, remap_weight,
+    out,
+    gw, rw, other, halo, other_atm, ext, source, own_part, send_part, recv_part,
+    select, rhs, acc, outgoing, incoming, turned,
+    gw_sem, rw_sem, near_send, near_recv, part_send, part_recv, red_send, red_recv,
+):
+    me, core = lax.axis_index("dom"), lax.axis_index("field")
+    fields, width = ocean.shape
+    nblocks, stencil, block_len, grad_len = gw.shape
+    tiles, depth, cells = rw.shape
+    rows = devices * owned
+    span = fields // groups * cells
+    peer = (me, 1 - core)
+    gw_parts, rw_parts, c_parts = gw_sem.shape[0], rw_sem.shape[0], part_send.shape[0]
+    gw_step, rw_step, c_step = nblocks // gw_parts, tiles // rw_parts, tiles // c_parts
+
+    gw_copies = [
+        pltpu.make_async_copy(
+            grad_weight.at[pl.ds(i * gw_step, gw_step)],
+            gw.at[pl.ds(i * gw_step, gw_step)],
+            gw_sem.at[i],
+        )
+        for i in range(gw_parts)
+    ]
+    rw_copies = [
+        pltpu.make_async_copy(
+            remap_weight.at[pl.ds(i * rw_step, rw_step)],
+            rw.at[pl.ds(i * rw_step, rw_step)],
+            rw_sem.at[i],
+        )
+        for i in range(rw_parts)
+    ]
+    for copy in gw_copies + rw_copies:
+        copy.start()
+
+    masks = stage_masks(stages, core)
+    has_left, has_right = me > 0, me < devices - 1
+    barrier = pltpu.get_barrier_semaphore()
+
+    def greet(target):
+        pl.semaphore_signal(barrier, inc=1, device_id=target, device_id_type=MESH)
+
+    greet(peer)
+    for mask in masks:
+        greet((me ^ mask, core))
+
+    @pl.when(has_left)
+    def _():
+        greet((me - 1, core))
+        greet((me - 1, 1 - core))
+
+    @pl.when(has_right)
+    def _():
+        greet((me + 1, core))
+        greet((me + 1, 1 - core))
+
+    sides = jnp.minimum(me, 1) + jnp.minimum(devices - 1 - me, 1)
+    pl.semaphore_wait(barrier, 1 + stages + 2 * sides)
+
+    def remote(src, dst, send, recv, target):
+        return pltpu.make_async_remote_copy(
+            src_ref=src, dst_ref=dst, send_sem=send, recv_sem=recv,
+            device_id=target, device_id_type=MESH,
+        )
+
+    edge = HALO * block_len
+    first = ocean.at[:, pl.ds(0, edge)]
+    last = ocean.at[:, pl.ds(width - edge, edge)]
+    left_copies = [
+        remote(first, halo.at[1, g], near_send.at[g], near_recv.at[2 + g], (me - 1, (core + g) % 2))
+        for g in range(2)
+    ]
+    right_copies = [
+        remote(last, halo.at[0, g], near_send.at[2 + g], near_recv.at[g], (me + 1, (core + g) % 2))
+        for g in range(2)
+    ]
+
+    @pl.when(has_left)
+    def _():
+        for copy in left_copies:
+            copy.start()
+
+    @pl.when(has_right)
+    def _():
+        for copy in right_copies:
+            copy.start()
+
+    ocean_copy = remote(ocean, other, near_send.at[4], near_recv.at[4], peer)
+    ocean_copy.start()
+    atm_copy = remote(tile_atm, other_atm, near_send.at[5], near_recv.at[5], peer)
+    atm_copy.start()
+
+    half_rows = ext.shape[1] // 2
+
+    def spread(data, block, group):
+        low = group * half_rows
+        ext[block, pl.ds(low, fields), :] = data
+
+    for b in range(nblocks):
+        spread(ocean[:, pl.ds(b * block_len, block_len)], HALO + b, 0)
+    slot = atm_owner[...]
+    away = (slot // owned) ^ me
+    bits = [(away >> s) & 1 for s in range(stages)]
+    if stages >= 2:
+        zero, one = bits[0], bits[1]
+        bits[0] = jnp.where(core == 0, zero, one)
+        bits[1] = jnp.where(core == 0, one, zero)
+    rank = bits[0] * 0
+    for bit in bits:
+        rank = rank * 2 + bit
+    rel = rank * owned + slot % owned
+    ocean_copy.wait_recv()
+    for b in range(nblocks):
+        spread(other[:, pl.ds(b * block_len, block_len)], HALO + b, 1)
+    atm_copy.wait_recv()
+    atm_tiles = atm_owner.shape[1]
+    owner_hot = (lax.broadcasted_iota(jnp.int32, (rows, atm_tiles), 0) == rel).astype(
+        jnp.float32
+    ).astype(jnp.bfloat16)
+    ids = lax.broadcasted_iota(jnp.int32, (atm_tiles, tiles), 0)
+    tile_hot = jnp.concatenate(
+        [
+            (ids == tile_atm[...]).astype(jnp.float32),
+            (ids == other_atm[...]).astype(jnp.float32),
+        ],
+        axis=1,
+    ).astype(jnp.bfloat16)
+    chosen = jnp.dot(owner_hot, tile_hot, preferred_element_type=jnp.float32)
+    select[:, : 2 * tiles] = chosen.astype(jnp.bfloat16)
+    select[:, 2 * tiles :] = chosen[:, :tiles].astype(jnp.bfloat16)
+
+    @pl.when(has_right)
+    def _():
+        for g in range(2):
+            left_copies[g].wait_recv()
+            for b in range(HALO):
+                spread(halo[1, g, :, pl.ds(b * block_len, block_len)], HALO + nblocks + b, g)
+
+    @pl.when(has_left)
+    def _():
+        for g in range(2):
+            right_copies[g].wait_recv()
+            for b in range(HALO):
+                spread(halo[0, g, :, pl.ds(b * block_len, block_len)], b, g)
+
+    base = me * nblocks
+    for i in range(gw_parts):
+        gw_copies[i].wait()
+
+        def gradient(j, _, i=i):
+            b = i * gw_step + j
+            picked = [ext[jnp.clip(neighbours[k, b] - base + HALO, 0, nblocks + 2 * HALO - 1)] for k in range(stencil)]
+            weights = gw[b].reshape(stencil * block_len, grad_len)
+            grad = jnp.dot(
+                jnp.concatenate(picked, axis=1), weights, preferred_element_type=jnp.float32
+            )
+            source[b, :, :block_len] = ext[HALO + b]
+            source[b, :, block_len:] = grad.astype(jnp.bfloat16)
+            return 0
+
+        lax.fori_loop(0, gw_step, gradient, 0, unroll=True)
+
+    part_copies = []
+    loads_per = rw_parts // c_parts
+    for i in range(c_parts):
+        for j in range(loads_per):
+            rw_copies[i * loads_per + j].wait()
+
+        def contribute(j, _, i=i):
+            t = i * c_step + j
+            value = jnp.dot(
+                source[jnp.clip(tile_src[t] - base, 0, nblocks - 1)], rw[t], preferred_element_type=jnp.float32
+            )
+            own_part[pl.ds(t * half_rows, half_rows), :] = value[:half_rows]
+            send_part[t] = value[half_rows:].astype(jnp.bfloat16)
+            return 0
+
+        lax.fori_loop(0, c_step, contribute, 0, unroll=8)
+        copy = remote(
+            send_part.at[pl.ds(i * c_step, c_step)],
+            recv_part.at[pl.ds(i * c_step, c_step)],
+            part_send.at[i], part_recv.at[i], peer,
+        )
+        copy.start()
+        part_copies.append(copy)
+
+    for f in range(fields):
+        g, at = f // (fields // groups), f % (fields // groups)
+        mine = own_part[pl.ds(f, tiles, stride=half_rows), :]
+        high = mine.astype(jnp.bfloat16)
+        low = (mine - high.astype(jnp.float32)).astype(jnp.bfloat16)
+        rhs[g, :tiles, at * cells : (at + 1) * cells] = high
+        rhs[g, 2 * tiles :, at * cells : (at + 1) * cells] = low
+    for i in range(c_parts):
+        part_copies[i].wait_recv()
+        own_part[pl.ds((tiles + i * c_step) * half_rows, c_step * half_rows), :] = (
+            recv_part[pl.ds(i * c_step, c_step)]
+            .astype(jnp.float32)
+            .reshape(c_step * half_rows, cells)
+        )
+
+    def reduction(g, s):
+        part = rows >> (s + 1)
+        return remote(
+            outgoing.at[g, pl.ds(part, part)], incoming.at[g, pl.ds(part, part)],
+            red_send.at[g, s], red_recv.at[g, s], (me ^ masks[s], core),
+        )
+
+    per = fields // groups
+    for g in range(groups):
+        for at in range(per):
+            theirs = own_part[pl.ds(tiles * half_rows + g * per + at, tiles, stride=half_rows), :]
+            rhs[g, tiles : 2 * tiles, at * cells : (at + 1) * cells] = theirs.astype(jnp.bfloat16)
+        outgoing[g, rows // 2 :] = jnp.dot(
+            select[rows // 2 :], rhs[g], preferred_element_type=jnp.float32
+        ).astype(jnp.bfloat16)
+        reduction(g, 0).start()
+    for g in range(groups):
+        acc[g] = jnp.dot(select[: rows // 2], rhs[g], preferred_element_type=jnp.float32)
+    for s in range(stages):
+        part = rows >> (s + 1)
+        for g in range(groups):
+            reduction(g, s).wait_recv()
+            if s < stages - 1:
+                quarter = part // 2
+                outgoing[g, quarter:part] = (
+                    acc[g, quarter:part] + incoming[g, part + quarter : 2 * part].astype(jnp.float32)
+                ).astype(jnp.bfloat16)
+                reduction(g, s + 1).start()
+                acc[g, :quarter] += incoming[g, part : part + quarter].astype(jnp.float32)
+            else:
+                final = acc[g, :part] + incoming[g, part : 2 * part].astype(jnp.float32)
+                for at in range(per):
+                    turned[pl.ds((g * per + at) * owned, owned), :] = final[
+                        :, at * cells : (at + 1) * cells
+                    ]
+    for a in range(owned):
+        out[:, pl.ds(a * cells, cells)] = turned[pl.ds(a, fields, stride=owned), :]
+
+    @pl.when(has_left)
+    def _():
+        for copy in left_copies:
+            copy.wait_send()
+
+    @pl.when(has_right)
+    def _():
+        for copy in right_copies:
+            copy.wait_send()
+
+    ocean_copy.wait_send()
+    atm_copy.wait_send()
+    for copy in part_copies:
+        copy.wait_send()
+    for s in range(stages):
+        for g in range(groups):
+            reduction(g, s).wait_send()
+
+
+def fused(ocean, grad_weight, neighbours, remap_weight, tile_src, tile_atm, atm_owner):
+    fields, width = ocean.shape
+    devices = lax.axis_size("dom")
+    stages = devices.bit_length() - 1
+    nblocks, _, block_len, grad_len = grad_weight.shape
+    tiles, depth, cells = remap_weight.shape
+    owned = atm_owner.shape[0] // devices
+    rows = devices * owned
+    groups = 3 if fields % 3 == 0 else 1
+    span = fields // groups * cells
+    half = -(-fields // 16) * 16
+    bf16, f32 = jnp.bfloat16, jnp.float32
+    dma = pltpu.SemaphoreType.DMA
+    vmem = pl.BlockSpec(memory_space=pltpu.VMEM)
+    smem = pl.BlockSpec(memory_space=pltpu.SMEM)
+    anyspace = pl.BlockSpec(memory_space=pl.ANY)
+    return pl.pallas_call(
+        functools.partial(fused_kernel, devices, stages, owned, groups),
+        out_shape=jax.ShapeDtypeStruct((fields, owned * cells), f32),
+        in_specs=[vmem, smem, smem, vmem, vmem, anyspace, anyspace],
+        out_specs=vmem,
+        scratch_shapes=[
+            pltpu.VMEM(grad_weight.shape, bf16),
+            pltpu.VMEM(remap_weight.shape, bf16),
+            pltpu.VMEM((fields, width), bf16),
+            pltpu.VMEM((2, 2, fields, HALO * block_len), bf16),
+            pltpu.VMEM((1, tiles), jnp.int32),
+            pltpu.VMEM((nblocks + 2 * HALO, 2 * half, block_len), bf16),
+            pltpu.VMEM((nblocks, 2 * half, depth), bf16),
+            pltpu.VMEM((2 * tiles * half, cells), f32),
+            pltpu.VMEM((tiles, half, cells), bf16),
+            pltpu.VMEM((tiles, half, cells), bf16),
+            pltpu.VMEM((rows, 3 * tiles), bf16),
+            pltpu.VMEM((groups, 3 * tiles, span), bf16),
+            pltpu.VMEM((groups, rows // 2, span), f32),
+            pltpu.VMEM((groups, rows, span), bf16),
+            pltpu.VMEM((groups, rows, span), bf16),
+            pltpu.VMEM((fields * owned, cells), f32),
+            dma((4,)), dma((8,)), dma((6,)), dma((6,)), dma((4,)), dma((4,)),
+            dma((groups, stages)), dma((groups, stages)),
+        ],
+        compiler_params=pltpu.CompilerParams(
+            collective_id=0, has_side_effects=True, vmem_limit_bytes=60 * 2**20
+        ),
+    )(
+        ocean, neighbours.T, tile_src, tile_atm.reshape(1, -1), atm_owner.reshape(1, -1),
+        grad_weight, remap_weight,
+    )
+
+
+def plan(ocean, grad_weight, neighbours, remap_weight, tile_src, tile_atm, atm_owner):
+    devices = lax.axis_size("dom")
+    atm_tiles = atm_owner.shape[0]
+    power = devices > 1 and devices & (devices - 1) == 0
+    small = atm_tiles * ocean.shape[0] * remap_weight.shape[2] <= 2**20
+    even = (atm_tiles // devices) % 16 == 0 and lax.axis_size("field") == 2
+    body = fused if power and small and even else local
+    return body(ocean, grad_weight, neighbours, remap_weight, tile_src, tile_atm, atm_owner)
+
+
 def solution(mesh):
     in_specs = (
         P("field", "dom"),
@@ -95,4 +431,4 @@
         P(),
     )
     out_specs = P("field", "dom")
-    return jax.shard_map(local, mesh=mesh, in_specs=in_specs, out_specs=out_specs, check_vma=False)
+    return jax.shard_map(plan, mesh=mesh, in_specs=in_specs, out_specs=out_specs, check_vma=False)

time: 154 us -> 35.4 us (0.23)
  the two profiles are of different devices: /device:TPU:15 before, /device:TPU:0 now
where the time goes in v1:
time: 35.4 us; the launch traced here: 35.2 us
  Pallas kernels  33.6 us (95%)
  local copies, waits for them, and re-layouts  1.57 us (4%)
    pallas_call x1, Pallas kernels, fused(): pl.pallas_call(functools.partial(fused_kernel, devices, stages, owned, gr...  33.6 us
    unnamed x1, local copies, waits for them, and re-layouts  1.57 us

profile of v1, /device:TPU:0, one launch (start us, length us, event | category | flops | bytes accessed | tf_op | source)
XLA Modules:
  0.0 35.2 jit_solution(10705709921949089397)
XLA Ops:
  0.0 33.6 %shard_map.73 = f32[15,2048]{1,0:T(8,128)} custom-call(bf16[15,2048]{1,0:T(8,128)(2,1)} %ocean.1, s32[4,16]{1,0:T(4,128)} %bitcast.3, s32[64]{0:T(128)} %tile_src.1, s32[1,64]{1,0:T(1,128)} %bitcast.5, s32[1,256]{1,0:T(1,128)} %bitcast.4, bf16[16,4,128,256]{3,2,1,0:T(8,128)(2,1)} %grad_weight.1, bf16[64,384,128]{2,1,0:T(8,128)(2,1)} %remap_weight.1), custom_call_target="tpu_custom_call" | custom-call | tf_op jit(solution)/shard_map/pallas_call | solution.py:379
  33.6 1.6 %copy.9 = f32[15,2048]{1,0:T(8,128)} copy(f32[15,2048]{1,0:T(8,128)} %shard_map.73) | data formatting | bytes 245760

commit v2 on v1

--- a/solution.py
+++ b/solution.py
@@ -92,12 +92,16 @@
 MESH = pl.DeviceIdType.MESH
 
 
-def stage_masks(stages, core):
-    masks = [jnp.int32(1 << s) for s in range(stages)]
-    if stages >= 2:
-        masks[0] = jnp.where(core == 0, 1, 2)
-        masks[1] = jnp.where(core == 0, 2, 1)
-    return masks
+def stage_bits(stages, kind, core):
+    order = list(range(stages))
+    if kind == 1:
+        order = [2, 0, 1] + order[3:]
+    swapped = [{0: 1, 1: 0}.get(b, b) for b in order] if stages >= 2 else order
+    return [jnp.where(core == 0, a, b) if a != b else a for a, b in zip(order, swapped)]
+
+
+def kind_of(group, groups, stages):
+    return 1 if group == 1 and groups > 2 and stages >= 3 else 0
 
 
 def fused_kernel(
@@ -137,7 +141,8 @@
     for copy in gw_copies + rw_copies:
         copy.start()
 
-    masks = stage_masks(stages, core)
+    kinds = [kind_of(g, groups, stages) for g in range(groups)]
+    bits_of = [stage_bits(stages, kind, core) for kind in range(max(kinds) + 1)]
     has_left, has_right = me > 0, me < devices - 1
     barrier = pltpu.get_barrier_semaphore()
 
@@ -145,8 +150,8 @@
         pl.semaphore_signal(barrier, inc=1, device_id=target, device_id_type=MESH)
 
     greet(peer)
-    for mask in masks:
-        greet((me ^ mask, core))
+    for s in range(stages):
+        greet((me ^ (1 << s), core))
 
     @pl.when(has_left)
     def _():
@@ -204,23 +209,17 @@
         spread(ocean[:, pl.ds(b * block_len, block_len)], HALO + b, 0)
     slot = atm_owner[...]
     away = (slot // owned) ^ me
-    bits = [(away >> s) & 1 for s in range(stages)]
-    if stages >= 2:
-        zero, one = bits[0], bits[1]
-        bits[0] = jnp.where(core == 0, zero, one)
-        bits[1] = jnp.where(core == 0, one, zero)
-    rank = bits[0] * 0
-    for bit in bits:
-        rank = rank * 2 + bit
-    rel = rank * owned + slot % owned
+    ranks = []
+    for bits in bits_of:
+        rank = away * 0
+        for bit in bits:
+            rank = rank * 2 + ((away >> bit) & 1)
+        ranks.append(rank * owned + slot % owned)
     ocean_copy.wait_recv()
     for b in range(nblocks):
         spread(other[:, pl.ds(b * block_len, block_len)], HALO + b, 1)
     atm_copy.wait_recv()
     atm_tiles = atm_owner.shape[1]
-    owner_hot = (lax.broadcasted_iota(jnp.int32, (rows, atm_tiles), 0) == rel).astype(
-        jnp.float32
-    ).astype(jnp.bfloat16)
     ids = lax.broadcasted_iota(jnp.int32, (atm_tiles, tiles), 0)
     tile_hot = jnp.concatenate(
         [
@@ -229,9 +228,15 @@
         ],
         axis=1,
     ).astype(jnp.bfloat16)
-    chosen = jnp.dot(owner_hot, tile_hot, preferred_element_type=jnp.float32)
-    select[:, : 2 * tiles] = chosen.astype(jnp.bfloat16)
-    select[:, 2 * tiles :] = chosen[:, :tiles].astype(jnp.bfloat16)
+    for kind, rel in enumerate(ranks):
+        owner_hot = (
+            (lax.broadcasted_iota(jnp.int32, (rows, atm_tiles), 0) == rel)
+            .astype(jnp.float32)
+            .astype(jnp.bfloat16)
+        )
+        chosen = jnp.dot(owner_hot, tile_hot, preferred_element_type=jnp.float32)
+        select[kind, :, : 2 * tiles] = chosen.astype(jnp.bfloat16)
+        select[kind, :, 2 * tiles :] = chosen[:, :tiles].astype(jnp.bfloat16)
 
     @pl.when(has_right)
     def _():
@@ -307,7 +312,7 @@
         part = rows >> (s + 1)
         return remote(
             outgoing.at[g, pl.ds(part, part)], incoming.at[g, pl.ds(part, part)],
-            red_send.at[g, s], red_recv.at[g, s], (me ^ masks[s], core),
+            red_send.at[g, s], red_recv.at[g, s], (me ^ (1 << bits_of[kinds[g]][s]), core),
         )
 
     per = fields // groups
@@ -316,28 +321,30 @@
             theirs = own_part[pl.ds(tiles * half_rows + g * per + at, tiles, stride=half_rows), :]
             rhs[g, tiles : 2 * tiles, at * cells : (at + 1) * cells] = theirs.astype(jnp.bfloat16)
         outgoing[g, rows // 2 :] = jnp.dot(
-            select[rows // 2 :], rhs[g], preferred_element_type=jnp.float32
+            select[kinds[g], rows // 2 :], rhs[g], preferred_element_type=jnp.float32
         ).astype(jnp.bfloat16)
         reduction(g, 0).start()
     for g in range(groups):
-        acc[g] = jnp.dot(select[: rows // 2], rhs[g], preferred_element_type=jnp.float32)
-    for s in range(stages):
+        acc[g] = jnp.dot(
+            select[kinds[g], : rows // 2], rhs[g], preferred_element_type=jnp.float32
+        )
+    steps = [(g, s) for s in range(stages) for g in range(groups)]
+    for g, s in sorted(steps, key=lambda step: (step[0] + 2.5 * step[1], step[1])):
         part = rows >> (s + 1)
-        for g in range(groups):
-            reduction(g, s).wait_recv()
-            if s < stages - 1:
-                quarter = part // 2
-                outgoing[g, quarter:part] = (
-                    acc[g, quarter:part] + incoming[g, part + quarter : 2 * part].astype(jnp.float32)
-                ).astype(jnp.bfloat16)
-                reduction(g, s + 1).start()
-                acc[g, :quarter] += incoming[g, part : part + quarter].astype(jnp.float32)
-            else:
-                final = acc[g, :part] + incoming[g, part : 2 * part].astype(jnp.float32)
-                for at in range(per):
-                    turned[pl.ds((g * per + at) * owned, owned), :] = final[
-                        :, at * cells : (at + 1) * cells
-                    ]
+        reduction(g, s).wait_recv()
+        if s < stages - 1:
+            quarter = part // 2
+            outgoing[g, quarter:part] = (
+                acc[g, quarter:part] + incoming[g, part + quarter : 2 * part].astype(jnp.float32)
+            ).astype(jnp.bfloat16)
+            reduction(g, s + 1).start()
+            acc[g, :quarter] += incoming[g, part : part + quarter].astype(jnp.float32)
+        else:
+            final = acc[g, :part] + incoming[g, part : 2 * part].astype(jnp.float32)
+            for at in range(per):
+                turned[pl.ds((g * per + at) * owned, owned), :] = final[
+                    :, at * cells : (at + 1) * cells
+                ]
     for a in range(owned):
         out[:, pl.ds(a * cells, cells)] = turned[pl.ds(a, fields, stride=owned), :]
 
@@ -371,6 +378,7 @@
     groups = 3 if fields % 3 == 0 else 1
     span = fields // groups * cells
     half = -(-fields // 16) * 16
+    kinds = 1 + max(kind_of(g, groups, stages) for g in range(groups))
     bf16, f32 = jnp.bfloat16, jnp.float32
     dma = pltpu.SemaphoreType.DMA
     vmem = pl.BlockSpec(memory_space=pltpu.VMEM)
@@ -392,7 +400,7 @@
             pltpu.VMEM((2 * tiles * half, cells), f32),
             pltpu.VMEM((tiles, half, cells), bf16),
             pltpu.VMEM((tiles, half, cells), bf16),
-            pltpu.VMEM((rows, 3 * tiles), bf16),
+            pltpu.VMEM((kinds, rows, 3 * tiles), bf16),
             pltpu.VMEM((groups, 3 * tiles, span), bf16),
             pltpu.VMEM((groups, rows // 2, span), f32),
             pltpu.VMEM((groups, rows, span), bf16),

time: 35.4 us -> 32.9 us (0.929)
  Pallas kernels: 33.6 us -> 31.2 us
    pallas_call x1, Pallas kernels: 33.6 us -> 31.2 us  [fused(): pl.pallas_call(functools.partial(fused_kernel, devices, stages, owned, gr...]
where the time goes in v2:
time: 32.9 us; the launch traced here: 32.8 us
  Pallas kernels  31.2 us (95%)
  local copies, waits for them, and re-layouts  1.57 us (5%)
    pallas_call x1, Pallas kernels, fused(): pl.pallas_call(functools.partial(fused_kernel, devices, stages, owned, gr...  31.2 us
    unnamed x1, local copies, waits for them, and re-layouts  1.57 us

profile of v2, /device:TPU:0, one launch (start us, length us, event | category | flops | bytes accessed | tf_op | source)
XLA Modules:
  0.0 32.8 jit_solution(10639245072568317432)
XLA Ops:
  0.0 31.2 %shard_map.73 = f32[15,2048]{1,0:T(8,128)} custom-call(bf16[15,2048]{1,0:T(8,128)(2,1)} %ocean.1, s32[4,16]{1,0:T(4,128)} %bitcast.3, s32[64]{0:T(128)} %tile_src.1, s32[1,64]{1,0:T(1,128)} %bitcast.5, s32[1,256]{1,0:T(1,128)} %bitcast.4, bf16[16,4,128,256]{3,2,1,0:T(8,128)(2,1)} %grad_weight.1, bf16[64,384,128]{2,1,0:T(8,128)(2,1)} %remap_weight.1), custom_call_target="tpu_custom_call" | custom-call | tf_op jit(solution)/shard_map/pallas_call | solution.py:387
  31.2 1.6 %copy.9 = f32[15,2048]{1,0:T(8,128)} copy(f32[15,2048]{1,0:T(8,128)} %shard_map.73) | data formatting | bytes 245760
